TPU v7x, 32 devices: a whole 2x2x4 slice. The times are simulated.
32 devices in a mesh: dp: 8 (over z, x), expert: 4 (over y, core).
Axes of the slice: x: 2, y: 2, z: 4, core: 2. Of those that a mesh axis runs over, the one named last changes fastest.
Arguments:
- tokens: bfloat16 [2, 8192, 1024], P(None, ('dp', 'expert')), may hold values from -6 to 6
- lengths: int32 [2, 8], P(None, 'dp'), may hold values from 256 to 1024, as said below
- routes: int32 [2, 8192, 2], P(None, ('dp', 'expert')), may hold values from 0 to 3, all different within a row
- w_qkv: bfloat16 [1024, 3072], P(('dp', 'expert')), may hold values from -0.1875 to 0.1875
- w_out: bfloat16 [1024, 1024], P(('dp', 'expert')), may hold values from -3 to 3
- norm_gains: bfloat16 [1024, 2], P(('dp', 'expert')), may hold values from 0.5 to 1.5
- bias_table: bfloat16 [512], P(('dp', 'expert')), may hold values from -4 to 4
- router: bfloat16 [1024, 4], P(('dp', 'expert')), may hold values from -0.09375 to 0.09375
- w_in: bfloat16 [4, 1024, 5632], P('expert', 'dp'), may hold values from -0.1875 to 0.1875
- w_down: bfloat16 [4, 2816, 1024], P('expert', 'dp'), may hold values from -0.4375 to 0.4375
- cotangent: bfloat16 [2, 8192, 1024], P(None, ('dp', 'expert')), may hold values from -6 to 6
Outputs:
- block_out: bfloat16 [2, 8192, 1024], P(None, ('dp', 'expert'))
- grad_tokens: float32 [2, 8192, 1024], P(None, ('dp', 'expert'))
- grad_qkv: float32 [1024, 3072], P(('dp', 'expert'))
- grad_out_proj: float32 [1024, 1024], P(('dp', 'expert'))
- grad_gains: float32 [1024, 2], P(('dp', 'expert'))
- grad_bias: float32 [512], P(('dp', 'expert'))
- grad_router: float32 [1024, 4], P(('dp', 'expert'))
- grad_w_in: float32 [4, 1024, 5632], P('expert', 'dp')
- grad_w_down: float32 [4, 2816, 1024], P('expert', 'dp')
Inputs may be any that keep to these rules, and one draw needn't show every extreme that they name: `lengths`: each sequence has at least 256 live tokens; some sequence is exactly 1024 long.
All inputs are finite; a program needn't handle non-finite values.
Results may differ from a plain program's by a relative error of at most 0.02.
Values may be sent and summed in bfloat16 or wider, within the bound.
A program may use at most 320 MiB of HBM per device.

v0:
```python
import jax
import jax.numpy as jnp
from jax import lax
from jax.sharding import PartitionSpec as P

D = 1024
H = 16
DH = 64
FF = 2816
BUCKETS = 32
TOP = 2
bucket_edges = (12, 16, 23, 32, 46, 64, 91)
norm_eps = 1e-06
highest = lax.Precision.HIGHEST


def bucket_ids(query_pos, key_pos):
    offset = key_pos[None, :] - query_pos[:, None]
    dist = jnp.abs(offset)
    beyond = jnp.zeros_like(dist)
    for edge in bucket_edges:
        beyond = beyond + (dist >= edge).astype(jnp.int32)
    near = jnp.where(dist < 8, dist, 8 + beyond)
    return near + 16 * (offset > 0).astype(jnp.int32)


def rms_scale(values, gain):
    return values * lax.rsqrt(jnp.mean(values * values, axis=-1, keepdims=True) + norm_eps) * gain


def geglu(joined):
    half = joined.shape[-1] // 2
    return jax.nn.gelu(joined[..., :half], approximate=True) * joined[..., half:]


def slot_tables(route_rows, live, experts, capacity):
    count, top = route_rows.shape
    picks = (route_rows[:, :, None] == jnp.arange(experts, dtype=jnp.int32)[None, None, :]).astype(
        jnp.int32
    ) * live[:, None, None]
    flat = picks.reshape(count * top, experts)
    before = jnp.cumsum(flat, axis=0) - flat
    place = jnp.sum(before * flat, axis=1).reshape(count, top)
    kept = (place < capacity) & (live[:, None] > 0)
    target = jnp.where(kept, route_rows * capacity + place, -1)
    columns = jnp.arange(experts * capacity, dtype=jnp.int32)
    return target[:, :, None] == columns[None, None, :]


def matmul(left, right):
    return jnp.dot(left, right, preferred_element_type=jnp.float32)


def inner_rows(left, right):
    return jnp.einsum("ti,tj->ij", left, right, preferred_element_type=jnp.float32)


def times_trans(left, right):
    return jnp.einsum("ti,ji->tj", left, right, preferred_element_type=jnp.float32)


def local(
    tokens, lengths, routes, w_qkv, w_out, norm_gains, bias_table, router, w_in, w_down, cotangent
):
    micro, rows, width = tokens.shape
    experts = lax.axis_size("expert")
    seq_len = rows * experts
    capacity = (5 * rows * TOP + 4 * experts - 1) // (4 * experts)
    scale = DH ** (-0.5)
    query_pos = lax.axis_index("expert") * rows + jnp.arange(rows, dtype=jnp.int32)
    key_pos = jnp.arange(seq_len, dtype=jnp.int32)
    bucket_hot = (
        bucket_ids(query_pos, key_pos)[:, :, None]
        == jnp.arange(BUCKETS, dtype=jnp.int32)[None, None, :]
    ).astype(jnp.float32)
    expert_hot = jnp.arange(experts, dtype=jnp.int32)
    acc_qkv = jnp.zeros((D, 3 * D), jnp.float32)
    acc_out = jnp.zeros((D, D), jnp.float32)
    acc_gains = jnp.zeros((D, 2), jnp.float32)
    acc_bias = jnp.zeros((BUCKETS, H), jnp.float32)
    acc_router = jnp.zeros((D, experts), jnp.float32)
    acc_in = jnp.zeros((D, 2 * FF), jnp.float32)
    acc_down = jnp.zeros((FF, D), jnp.float32)
    outputs = []
    input_grads = []
    for step in range(micro):
        (wqkv, wout, gains, table_flat, route_w), (win, wdown) = (
            (
                lax.all_gather(w_qkv, ("dp", "expert"), axis=0, tiled=True),
                lax.all_gather(w_out, ("dp", "expert"), axis=0, tiled=True),
                lax.all_gather(norm_gains, ("dp", "expert"), axis=0, tiled=True),
                lax.all_gather(bias_table, ("dp", "expert"), axis=0, tiled=True),
                lax.all_gather(router, ("dp", "expert"), axis=0, tiled=True),
            ),
            (
                lax.all_gather(w_in, "dp", axis=1, tiled=True),
                lax.all_gather(w_down, "dp", axis=1, tiled=True),
            ),
        )
        gains_f = gains.astype(jnp.float32)
        table = table_flat.astype(jnp.float32).reshape(BUCKETS, H)
        x_rows = tokens[step].astype(jnp.float32)
        length = lengths[step, 0]
        key_live = key_pos < length
        h1 = rms_scale(x_rows, gains_f[:, 0]).astype(jnp.bfloat16)
        qkv = matmul(h1, wqkv)
        query = qkv[:, :D].astype(jnp.bfloat16)
        keys_low = qkv[:, D : 2 * D].astype(jnp.bfloat16)
        values_low = qkv[:, 2 * D :].astype(jnp.bfloat16)
        keys_all, values_all = (
            lax.all_gather(keys_low, "expert", axis=0, tiled=True),
            lax.all_gather(values_low, "expert", axis=0, tiled=True),
        )
        query_heads = query.reshape(rows, H, DH)
        key_heads = keys_all.reshape(seq_len, H, DH)
        value_heads = values_all.reshape(seq_len, H, DH)
        bias = jnp.einsum("qkb,bh->hqk", bucket_hot, table, precision=highest)
        scores = (
            scale
            * jnp.einsum("qhd,khd->hqk", query_heads, key_heads, preferred_element_type=jnp.float32)
            + bias
        )
        scores = jnp.where(key_live[None, None, :], scores, -1e30)
        top_score = jnp.max(scores, axis=-1, keepdims=True)
        lse = top_score + jnp.log(jnp.sum(jnp.exp(scores - top_score), axis=-1, keepdims=True))
        probs = jnp.exp(scores - lse)
        probs_low = probs.astype(jnp.bfloat16)
        attended = jnp.einsum(
            "hqk,khd->qhd", probs_low, value_heads, preferred_element_type=jnp.float32
        )
        attended_low = attended.astype(jnp.bfloat16)
        attended_low = attended_low.reshape(rows, D)
        x_mid = x_rows + matmul(attended_low, wout)
        h2 = rms_scale(x_mid, gains_f[:, 1]).astype(jnp.bfloat16)
        logits = matmul(h2, route_w)
        route_probs = jax.nn.softmax(logits, axis=-1)
        chosen = routes[step]
        route_hot = (chosen[:, :, None] == expert_hot[None, None, :]).astype(jnp.float32)
        gates = jnp.sum(route_probs[:, None, :] * route_hot, axis=-1)
        live = (query_pos < length).astype(jnp.int32)
        slot_hot = slot_tables(chosen, live, experts, capacity)
        slot_low = slot_hot.astype(jnp.bfloat16)
        any_slot = jnp.sum(slot_low, axis=1)
        sent = jnp.einsum("ts,td->sd", any_slot, h2, preferred_element_type=jnp.float32).astype(
            jnp.bfloat16
        )
        arrived = lax.all_to_all(
            sent.reshape(experts, capacity, D), "expert", split_axis=0, concat_axis=0, tiled=True
        )
        arrived_rows = arrived.reshape(experts * capacity, D)
        joined = matmul(arrived_rows, win[0])
        acted = geglu(joined).astype(jnp.bfloat16)
        produced = matmul(acted, wdown[0]).astype(jnp.bfloat16)
        returned = lax.all_to_all(
            produced.reshape(experts, capacity, D),
            "expert",
            split_axis=0,
            concat_axis=0,
            tiled=True,
        )
        returned_rows = returned.reshape(experts * capacity, D)
        picked = jnp.einsum(
            "tks,sd->tkd", slot_low, returned_rows, preferred_element_type=jnp.float32
        )
        mixed = jnp.sum(gates[:, :, None] * picked, axis=1)
        outputs.append((x_mid + mixed).astype(jnp.bfloat16))
        grad_out = cotangent[step].astype(jnp.float32)
        grad_gates = jnp.sum(grad_out[:, None, :] * picked, axis=-1)
        weighted = gates[:, :, None] * grad_out[:, None, :]
        grad_returned = jnp.einsum(
            "tks,tkd->sd", slot_hot.astype(jnp.float32), weighted, precision=highest
        ).astype(jnp.bfloat16)
        grad_produced = lax.all_to_all(
            grad_returned.reshape(experts, capacity, D),
            "expert",
            split_axis=0,
            concat_axis=0,
            tiled=True,
        )
        grad_produced = grad_produced.reshape(experts * capacity, D)
        acc_down = acc_down + inner_rows(acted, grad_produced)
        grad_acted = times_trans(grad_produced, wdown[0])
        geglu_pull = jax.vjp(geglu, joined)[1]
        grad_joined = geglu_pull(grad_acted)[0].astype(jnp.bfloat16)
        acc_in = acc_in + inner_rows(arrived_rows, grad_joined)
        grad_arrived = times_trans(grad_joined, win[0]).astype(jnp.bfloat16)
        grad_sent = lax.all_to_all(
            grad_arrived.reshape(experts, capacity, D),
            "expert",
            split_axis=0,
            concat_axis=0,
            tiled=True,
        )
        grad_h2 = jnp.einsum(
            "ts,sd->td",
            any_slot,
            grad_sent.reshape(experts * capacity, D),
            preferred_element_type=jnp.float32,
        )
        grad_route = jnp.sum(grad_gates[:, :, None] * route_hot, axis=1)
        grad_logits = route_probs * (
            grad_route - jnp.sum(route_probs * grad_route, axis=-1, keepdims=True)
        )
        grad_logits = grad_logits.astype(jnp.bfloat16)
        acc_router = acc_router + inner_rows(h2, grad_logits)
        grad_h2 = grad_h2 + times_trans(grad_logits, route_w)
        norm_pull = jax.vjp(rms_scale, x_mid, gains_f[:, 1])[1]
        grad_mid, grad_gain_two = norm_pull(grad_h2)
        grad_mid = grad_mid + grad_out
        grad_mid_low = grad_mid.astype(jnp.bfloat16)
        acc_out = acc_out + inner_rows(attended_low, grad_mid_low)
        grad_attended = times_trans(grad_mid_low, wout).astype(jnp.bfloat16).reshape(rows, H, DH)
        again = (
            scale
            * jnp.einsum("qhd,khd->hqk", query_heads, key_heads, preferred_element_type=jnp.float32)
            + bias
        )
        again = jnp.where(key_live[None, None, :], again, -1e30)
        probs_again = jnp.exp(again - lse)
        grad_values = jnp.einsum(
            "hqk,qhd->khd",
            probs_again.astype(jnp.bfloat16),
            grad_attended,
            preferred_element_type=jnp.float32,
        )
        grad_probs = jnp.einsum(
            "qhd,khd->hqk", grad_attended, value_heads, preferred_element_type=jnp.float32
        )
        weight_sum = jnp.sum(probs_again * grad_probs, axis=-1, keepdims=True)
        grad_scores = (probs_again * (grad_probs - weight_sum)).astype(jnp.bfloat16)
        grad_query = (
            scale
            * jnp.einsum("hqk,khd->qhd", grad_scores, key_heads, preferred_element_type=jnp.float32)
        ).astype(jnp.bfloat16)
        grad_keys = scale * jnp.einsum(
            "hqk,qhd->khd", grad_scores, query_heads, preferred_element_type=jnp.float32
        )
        acc_bias = acc_bias + jnp.einsum(
            "hqk,qkb->bh", grad_scores.astype(jnp.float32), bucket_hot, precision=highest
        )
        key_grads, value_grads = (
            lax.psum_scatter(
                grad_keys.reshape(seq_len, D).astype(jnp.bfloat16),
                "expert",
                scatter_dimension=0,
                tiled=True,
            ).astype(jnp.float32),
            lax.psum_scatter(
                grad_values.reshape(seq_len, D).astype(jnp.bfloat16),
                "expert",
                scatter_dimension=0,
                tiled=True,
            ).astype(jnp.float32),
        )
        grad_qkv = jnp.concatenate(
            [
                grad_query.reshape(rows, D),
                key_grads.astype(jnp.bfloat16),
                value_grads.astype(jnp.bfloat16),
            ],
            axis=1,
        )
        acc_qkv = acc_qkv + inner_rows(h1, grad_qkv)
        grad_h1 = times_trans(grad_qkv, wqkv)
        first_pull = jax.vjp(rms_scale, x_rows, gains_f[:, 0])[1]
        grad_x, grad_gain_one = first_pull(grad_h1)
        acc_gains = acc_gains + jnp.stack([grad_gain_one, grad_gain_two], axis=1)
        input_grads.append(grad_x + grad_mid)
    block_parts = (
        lax.psum_scatter(acc_qkv, ("dp", "expert"), scatter_dimension=0, tiled=True),
        lax.psum_scatter(acc_out, ("dp", "expert"), scatter_dimension=0, tiled=True),
        lax.psum_scatter(acc_gains, ("dp", "expert"), scatter_dimension=0, tiled=True),
        lax.psum_scatter(
            acc_bias.reshape(BUCKETS * H), ("dp", "expert"), scatter_dimension=0, tiled=True
        ),
        lax.psum_scatter(acc_router, ("dp", "expert"), scatter_dimension=0, tiled=True),
    )
    expert_parts = (
        lax.psum_scatter(
            acc_in[None].astype(jnp.bfloat16), "dp", scatter_dimension=1, tiled=True
        ).astype(jnp.float32),
        lax.psum_scatter(
            acc_down[None].astype(jnp.bfloat16), "dp", scatter_dimension=1, tiled=True
        ).astype(jnp.float32),
    )
    return (
        jnp.stack(outputs, axis=0),
        jnp.stack(input_grads, axis=0),
        block_parts[0],
        block_parts[1],
        block_parts[2],
        block_parts[3],
        block_parts[4],
        expert_parts[0],
        expert_parts[1],
    )


def solution(mesh):
    in_specs = (
        P(None, ("dp", "expert"), None),
        P(None, "dp"),
        P(None, ("dp", "expert"), None),
        P(("dp", "expert"), None),
        P(("dp", "expert"), None),
        P(("dp", "expert"), None),
        P(("dp", "expert")),
        P(("dp", "expert"), None),
        P("expert", "dp", None),
        P("expert", "dp", None),
        P(None, ("dp", "expert"), None),
    )
    out_specs = (
        P(None, ("dp", "expert"), None),
        P(None, ("dp", "expert"), None),
        P(("dp", "expert"), None),
        P(("dp", "expert"), None),
        P(("dp", "expert"), None),
        P(("dp", "expert")),
        P(("dp", "expert"), None),
        P("expert", "dp", None),
        P("expert", "dp", None),
    )
    return jax.shard_map(local, mesh=mesh, in_specs=in_specs, out_specs=out_specs, check_vma=False)
```

profile of v0, /device:TPU:0, one launch (start us, length us, event | category | flops | bytes accessed | tf_op | source)
XLA Modules:
  0.0 1743.3 jit_solution(17928922391032202754)
XLA Ops:
  8.0 43.5 %all-gather = bf16[32,32,2]{1,2,0:T(2,128)(2,1)S(1)} all-gather(bf16[1,32,2]{1,2,0:T(2,128)(2,1)} %bitcast.309), channel_id=1, replica_groups=mesh['dp'=8,'expert'=4] {'dp','expert'}, dimensions={0}, use_global_device_ids=true | all-gather | bytes 4224 | tf_op jit(solution)/shard_map/all_gather | solution.py:91
  53.1 29.9 %all-gather.11.cloned.1.call-done = bf16[1024,3072]{1,0:T(8,128)(2,1)} async-done(((bf16[32,3072]{1,0:T(8,128)(2,1)}), bf16[1024,3072]{1,0:T(8,128)(2,1)}) %all-gather.11.cloned.1.call-update) | async-done | bytes 6291472 | tf_op jit(solution)/shard_map/all_gather | solution.py:89
  114.2 46.5 %copy.135 = pred[256,1024,32]{1,2,0:T(32,128)(4,1)} copy(pred[256,1024,32]{0,2,1:T(32,128)(4,1)} %iota_compare_fusion) | data formatting | bytes 16777216 | tf_op jit(solution)/shard_map/eq | solution.py:73
  161.0 39.7 %all-reduce.4 = bf16[512]{0:T(512)(128)(2,1)S(1)} all-reduce(bf16[512]{0:T(512)(128)(2,1)S(1)} %dynamic-update-slice), channel_id=1, replica_groups=mesh['dp'=8,'expert'=4] {'dp','expert'}, use_global_device_ids=true, to_apply=%add.4 | all-reduce | flops 512 | bytes 2048
  204.2 40.5 %all-gather.1 = bf16[32,32,4]{1,2,0:T(4,128)(2,1)S(1)} all-gather(bf16[1,32,4]{1,2,0:T(4,128)(2,1)S(1)} %bitcast.308), channel_id=1, replica_groups=mesh['dp'=8,'expert'=4] {'dp','expert'}, dimensions={0}, use_global_device_ids=true | all-gather | bytes 8448 | tf_op jit(solution)/shard_map/all_gather | solution.py:93
  269.6 22.4 %fusion.171 = (f32[16,256]{1,0:T(8,128)S(1)}, f32[16,256,1024]{2,1,0:T(8,128)}) fusion(f32[16,256,1024]{2,0,1:T(8,128)} %fusion.142, bf16[256,16,64]{0,2,1:T(8,128)(2,1)} %bitcast.260, bf16[1024,16,64]{0,2,1:T(8,128)(2,1)S(1)} %bitcast.250, pred[1024]{0:T(1024)(128)(4,1)S(1)} %iota_compare_fusion.22), kind=kOutput, calls=%fused_computation.267 | convolution fusion | flops 553644032 | bytes 36193280 | tf_op jit(solution)/shard_map/qhd,khd->hqk/dot_general | solution.py:120
  322.8 22.4 %fusion.173 = (f32[16,256]{1,0:T(8,128)S(1)}, f32[16,256,1024]{2,1,0:T(8,128)}) fusion(f32[16,256,1024]{2,0,1:T(8,128)} %fusion.142, bf16[256,16,64]{0,2,1:T(8,128)(2,1)} %bitcast.262, bf16[1024,16,64]{0,2,1:T(8,128)(2,1)S(1)} %bitcast.252, pred[1024]{0:T(1024)(128)(4,1)S(1)} %iota_compare_fusion.21), kind=kOutput, calls=%fused_computation.269 | convolution fusion | flops 553644032 | bytes 36193280 | tf_op jit(solution)/shard_map/qhd,khd->hqk/dot_general | solution.py:120
  365.0 42.5 %all-gather.19.cloned.1.call-done = bf16[1,1024,5632]{2,1,0:T(8,128)(2,1)} async-done(((bf16[1,128,5632]{2,1,0:T(8,128)(2,1)}), bf16[1,1024,5632]{2,1,0:T(8,128)(2,1)}) %all-gather.19.cloned.1.call-update) | async-done | bytes 11534352 | tf_op jit(solution)/shard_map/all_gather | solution.py:96
  421.2 79.0 %all-gather.21.cloned.1.call-done = bf16[1,2816,1024]{2,1,0:T(8,128)(2,1)} async-done(((bf16[1,352,1024]{2,1,0:T(8,128)(2,1)}), bf16[1,2816,1024]{2,1,0:T(8,128)(2,1)}) %all-gather.21.cloned.1.call-update) | async-done | bytes 5767184 | tf_op jit(solution)/shard_map/all_gather | solution.py:97
  500.2 18.8 %fusion.36 = (f32[640,2816]{1,0:T(8,128)}, f32[640,2816]{1,0:T(8,128)}, bf16[640,2816]{1,0:T(8,128)(2,1)}) fusion(f32[640,5632]{1,0:T(8,128)} %fusion.12, bf16[640,1024]{1,0:T(8,128)(2,1)S(1)} %bitcast.282, bf16[1,2816,1024]{2,1,0:T(8,128)(2,1)} %all-gather.21.cloned.1.call-done), kind=kOutput, calls=%fused_computation.67 | convolution fusion | flops 3734241280 | bytes 39518208 | tf_op jit(solution)/shard_map/ti,ji->tj/dot_general | solution.py:59
  519.1 15.5 fusion.66
  613.4 13.8 fusion.10
  630.7 17.9 %fusion.37 = (f32[640,2816]{1,0:T(8,128)}, f32[640,2816]{1,0:T(8,128)}, bf16[640,2816]{1,0:T(8,128)(2,1)}) fusion(f32[640,5632]{1,0:T(8,128)} %fusion.10, bf16[640,1024]{1,0:T(8,128)(2,1)} %bitcast.58, bf16[1,2816,1024]{2,1,0:T(8,128)(2,1)} %all-gather.21.cloned.1.call-done), kind=kOutput, calls=%fused_computation.68 | convolution fusion | flops 3734241280 | bytes 39518208 | tf_op jit(solution)/shard_map/ti,ji->tj/dot_general | solution.py:59
  648.6 15.5 fusion.69
  693.1 14.3 all-to-all-done.3
  822.5 34.2 %reduce-scatter.15.cloned.1.call-done = bf16[256,1024]{0,1:T(8,128)(2,1)} async-done(((bf16[1024,1024]{0,1:T(8,128)(2,1)}), bf16[256,1024]{0,1:T(8,128)(2,1)}) %reduce-scatter.15.cloned.1.call-update) | async-done | bytes 524304 | tf_op jit(solution)/shard_map/reduce_scatter | solution.py:242
  877.3 19.1 %fusion.119 = f32[1024,5632]{1,0:T(8,128)} fusion(bf16[640,1024]{1,0:T(8,128)(2,1)} %bitcast.17, f32[640,2816]{1,0:T(8,128)} %get-tuple-element.26, f32[640,2816]{1,0:T(8,128)} %get-tuple-element.25), kind=kOutput, calls=%fused_computation.171 | convolution fusion | flops 7389184000 | bytes 38797312 | tf_op jit(solution)/shard_map/ti,tj->ij/dot_general | solution.py:55
  896.4 21.3 %fusion.14 = bf16[1,1024,5632]{2,1,0:T(8,128)(2,1)} fusion(f32[1024,5632]{1,0:T(8,128)} %fusion.119, bf16[640,1024]{1,0:T(8,128)(2,1)} %bitcast.36, f32[640,2816]{1,0:T(8,128)} %get-tuple-element.28, f32[640,2816]{1,0:T(8,128)} %get-tuple-element.27), kind=kOutput, calls=%fused_computation.33 | convolution fusion | flops 7400718336 | bytes 50331648 | tf_op jit(solution)/shard_map/ti,tj->ij/dot_general | solution.py:55
  972.3 39.4 %all-reduce.5 = f32[512]{0:T(512)S(1)} all-reduce(f32[512]{0:T(512)S(1)} %reshape.487), channel_id=9, replica_groups=mesh['dp'=8,'expert'=4] {'dp','expert'}, use_global_device_ids=true, to_apply=%region_47.48.clone | all-reduce | flops 512 | bytes 4096
  1019.6 109.5 %reduce-scatter.31.cloned.1.call-done = f32[32,2]{1,0:T(8,128)} async-done(((f32[1024,2]{1,0:T(8,128)}), f32[32,2]{1,0:T(8,128)}) %reduce-scatter.31.cloned.1.call-update) | async-done | bytes 272
  1130.5 108.7 %reduce-scatter.29.cloned.1.call-done = bf16[1,352,1024]{2,1,0:T(8,128)(2,1)} async-done(((bf16[1,2816,1024]{2,1,0:T(8,128)(2,1)}), bf16[1,352,1024]{2,1,0:T(8,128)(2,1)}) %reduce-scatter.29.cloned.1.call-update) | async-done | bytes 720912 | tf_op jit(solution)/shard_map/reduce_scatter | solution.py:282
  1241.6 193.3 %reduce-scatter.27.cloned.1.call-done = bf16[1,128,5632]{2,1,0:T(8,128)(2,1)} async-done(((bf16[1,1024,5632]{2,1,0:T(8,128)(2,1)}), bf16[1,128,5632]{2,1,0:T(8,128)(2,1)}) %reduce-scatter.27.cloned.1.call-update) | async-done | bytes 1441808 | tf_op jit(solution)/shard_map/reduce_scatter | solution.py:279
  1438.1 140.8 %reduce-scatter.25.cloned.1.call-done = f32[32,1024]{1,0:T(8,128)} async-done(((f32[1024,1024]{1,0:T(8,128)}), f32[32,1024]{1,0:T(8,128)}) %reduce-scatter.25.cloned.1.call-update) | async-done | bytes 131088 | tf_op jit(solution)/shard_map/reduce_scatter | solution.py:271
  1578.9 157.2 %reduce-scatter.23.cloned.1.call-done = f32[32,3072]{1,0:T(8,128)} async-done(((f32[1024,3072]{1,0:T(8,128)}), f32[32,3072]{1,0:T(8,128)}) %reduce-scatter.23.cloned.1.call-update) | async-done | bytes 393232 | tf_op jit(solution)/shard_map/reduce_scatter | solution.py:270
  (381 shorter events, 441.7 us)
Async XLA Ops:
  7.2 75.8 %all-gather.11.cloned.1.call-start = ((), (), s32[]{:S(2)}) async-start(), calls=%async_computation.18 | async-start | bytes 6488064 | tf_op jit(solution)/shard_map/all_gather | solution.py:89
  7.9 254.9 %all-gather.13.cloned.1.call-start = ((), (), s32[]{:S(2)}) async-start(), calls=%async_computation.19 | async-start | bytes 2621440 | tf_op jit(solution)/shard_map/all_gather | solution.py:112
  89.0 177.7 %all-gather.15.cloned.1.call-start = ((), (), s32[]{:S(2)}) async-start(), calls=%async_computation.20 | async-start | bytes 2621440 | tf_op jit(solution)/shard_map/all_gather | solution.py:111
  89.8 218.7 %all-gather.17.cloned.1.call-start = ((), (), s32[]{:S(2)}) async-start(), calls=%async_computation.21 | async-start | bytes 2162688 | tf_op jit(solution)/shard_map/all_gather | solution.py:90
  90.3 229.6 %all-gather.25.cloned.1.call-start = ((), (), s32[]{:S(2)}) async-start(), calls=%async_computation.25 | async-start | bytes 2621440 | tf_op jit(solution)/shard_map/all_gather | solution.py:111
  96.3 257.1 %all-gather.23.cloned.1.call-start = ((), (), s32[]{:S(2)}) async-start(), calls=%async_computation.24 | async-start | bytes 2621440 | tf_op jit(solution)/shard_map/all_gather | solution.py:112
  96.9 310.6 %all-gather.19.cloned.1.call-start = ((), (), s32[]{:S(2)}) async-start(), calls=%async_computation.22 | async-start | bytes 12976128 | tf_op jit(solution)/shard_map/all_gather | solution.py:96
  97.7 402.6 %all-gather.21.cloned.1.call-start = ((), (), s32[]{:S(2)}) async-start(), calls=%async_computation.23 | async-start | bytes 6488064 | tf_op jit(solution)/shard_map/all_gather | solution.py:97
  315.1 46.1 %all-to-all-start = ((bf16[4,160,1024]{2,1,0:T(8,128)(2,1)}), bf16[4,160,1024]{2,1,0:T(8,128)(2,1)}, u32[]{:S(2)}, u32[]{:S(2)}) async-start(bf16[4,160,1024]{2,1,0:T(8,128)(2,1)} %bitcast.16), calls=%async_computation | async-start | bytes 2621440 | tf_op jit(solution)/shard_map/all_to_all | solution.py:147
  361.3 139.0 %all-to-all-start.4 = ((bf16[4,160,1024]{2,1,0:T(8,128)(2,1)}), bf16[4,160,1024]{2,1,0:T(8,128)(2,1)S(1)}, u32[]{:S(2)}, u32[]{:S(2)}) async-start(bf16[4,160,1024]{2,1,0:T(8,128)(2,1)} %bitcast.286), calls=%async_computation.4 | async-start | bytes 2621440 | tf_op jit(solution)/shard_map/all_to_all | solution.py:173
  555.3 21.8 %all-to-all-start.1 = ((bf16[4,160,1024]{2,1,0:T(8,128)(2,1)}), bf16[4,160,1024]{2,1,0:T(8,128)(2,1)}, u32[]{:S(2)}, u32[]{:S(2)}) async-start(bf16[4,160,1024]{2,1,0:T(8,128)(2,1)} %bitcast.285), calls=%async_computation.1 | async-start | bytes 2621440 | tf_op jit(solution)/shard_map/all_to_all | solution.py:154
  608.7 22.0 %all-to-all-start.6 = ((bf16[4,160,1024]{2,1,0:T(8,128)(2,1)}), bf16[4,160,1024]{2,1,0:T(8,128)(2,1)}, u32[]{:S(2)}, u32[]{:S(2)}) async-start(bf16[4,160,1024]{2,1,0:T(8,128)(2,1)} %bitcast.287), calls=%async_computation.8 | async-start | bytes 2621440 | tf_op jit(solution)/shard_map/all_to_all | solution.py:173
  664.0 21.8 %all-to-all-start.7 = ((bf16[4,160,1024]{2,1,0:T(8,128)(2,1)}), bf16[4,160,1024]{2,1,0:T(8,128)(2,1)}, u32[]{:S(2)}, u32[]{:S(2)}) async-start(bf16[4,160,1024]{2,1,0:T(8,128)(2,1)} %bitcast.288), calls=%async_computation.9 | async-start | bytes 2621440 | tf_op jit(solution)/shard_map/all_to_all | solution.py:187
  685.8 21.6 %all-to-all-start.3 = ((bf16[4,160,1024]{2,1,0:T(8,128)(2,1)}), bf16[4,160,1024]{2,1,0:T(8,128)(2,1)}, u32[]{:S(2)}, u32[]{:S(2)}) async-start(bf16[4,160,1024]{2,1,0:T(8,128)(2,1)} %bitcast.284), calls=%async_computation.3 | async-start | bytes 2621440 | tf_op jit(solution)/shard_map/all_to_all | solution.py:154
  690.1 120.7 %reduce-scatter.21.cloned.1.call-start = ((), (), s32[]{:S(2)}) async-start(), calls=%async_computation.29 | async-start | bytes 2621440 | tf_op jit(solution)/shard_map/reduce_scatter | solution.py:248
  726.0 84.9 %reduce-scatter.19.cloned.1.call-start = ((), (), s32[]{:S(2)}) async-start(), calls=%async_computation.28 | async-start | bytes 2621440 | tf_op jit(solution)/shard_map/reduce_scatter | solution.py:242
  748.6 73.9 %reduce-scatter.17.cloned.1.call-start = ((), (), s32[]{:S(2)}) async-start(), calls=%async_computation.27 | async-start | bytes 2621440 | tf_op jit(solution)/shard_map/reduce_scatter | solution.py:248
  761.0 95.6 %reduce-scatter.15.cloned.1.call-start = ((), (), s32[]{:S(2)}) async-start(), calls=%async_computation.26 | async-start | bytes 2621440 | tf_op jit(solution)/shard_map/reduce_scatter | solution.py:242
  783.8 230.7 %reduce-scatter.33.cloned.1.call-start = ((), (), s32[]{:S(2)}) async-start(), calls=%async_computation.35 | async-start | bytes 540672
  810.8 318.4 %reduce-scatter.31.cloned.1.call-start = ((), (), s32[]{:S(2)}) async-start(), calls=%async_computation.34 | async-start | bytes 540672
  864.0 375.2 %reduce-scatter.29.cloned.1.call-start = ((), (), s32[]{:S(2)}) async-start(), calls=%async_computation.33 | async-start | bytes 6488064 | tf_op jit(solution)/shard_map/reduce_scatter | solution.py:282
  877.3 557.6 %reduce-scatter.27.cloned.1.call-start = ((), (), s32[]{:S(2)}) async-start(), calls=%async_computation.32 | async-start | bytes 12976128 | tf_op jit(solution)/shard_map/reduce_scatter | solution.py:279
  917.7 661.2 %reduce-scatter.25.cloned.1.call-start = ((), (), s32[]{:S(2)}) async-start(), calls=%async_computation.31 | async-start | bytes 4325376 | tf_op jit(solution)/shard_map/reduce_scatter | solution.py:271
  923.5 812.6 %reduce-scatter.23.cloned.1.call-start = ((), (), s32[]{:S(2)}) async-start(), calls=%async_computation.30 | async-start | bytes 12976128 | tf_op jit(solution)/shard_map/reduce_scatter | solution.py:270
  (85 other events, 2295.5 us)
Sparse Core Ops, SparseCore 0:
  10.9 72.0 all-gather.10
  89.1 21.0 all-gather.12
  112.4 22.5 all-gather.14
  137.7 56.5 all-gather.16
  196.3 21.4 all-gather.24
  219.2 22.6 all-gather.22
  244.2 163.3 all-gather.18
  409.7 90.4 all-gather.20
  726.1 28.4 reduce-scatter.20
  757.5 31.1 reduce-scatter.18
  791.3 31.1 reduce-scatter.16
  825.4 31.1 reduce-scatter.14
  858.9 135.8 reduce-scatter.32
  997.4 131.6 reduce-scatter.30
  1132.7 106.4 reduce-scatter.28
  1242.7 192.1 reduce-scatter.26
  1437.6 141.2 reduce-scatter.24
  1585.3 150.7 reduce-scatter.22
where the time goes:
time: 1750 us; the launch traced here: 1740 us
  waiting for transfers between devices  955 us (55%)
  matrix products  398 us (23%)
  blocking collectives  163 us (9%)
  local copies, waits for them, and re-layouts  107 us (6%)
  other arithmetic  68.2 us (4%)
  starting transfers between devices  36 us (2%)
    reduce_scatter x1, waiting for transfers between devices, local(): lax.psum_scatter(acc_in[None].astype(jnp.bfloat16), 'dp', scatter_dimensi...  193 us
    reduce_scatter x1, waiting for transfers between devices, local(): lax.psum_scatter(acc_qkv, ('dp', 'expert'), scatter_dimension=0, tiled=True)  157 us
    reduce_scatter x1, waiting for transfers between devices, local(): lax.psum_scatter(acc_out, ('dp', 'expert'), scatter_dimension=0, tiled=True)  141 us
    unnamed x20, waiting for transfers between devices  114 us
    reduce_scatter x1, waiting for transfers between devices, local(): lax.psum_scatter(acc_down[None].astype(jnp.bfloat16), 'dp', scatter_dimen...  109 us
    dot_general x10, matrix products, times_trans(): jnp.einsum('ti,ji->tj', left, right, preferred_element_type=jnp.float32)  88.5 us
    dot_general x10, matrix products, inner_rows(): jnp.einsum('ti,tj->ij', left, right, preferred_element_type=jnp.float32)  79.1 us
    unnamed x2, blocking collectives  79.1 us
  transfers between devices with their start and end apart: 26, of which 16 were waited for; matrix products, arithmetic and copies ran while one was open for 27% of the time, Pallas kernels for 0%

commit v1 on v0

--- a/solution.py
+++ b/solution.py
@@ -2,6 +2,7 @@
 import jax.numpy as jnp
 from jax import lax
 from jax.sharding import PartitionSpec as P
+from jax.lax import axis_index, axis_size, ppermute
 
 D = 1024
 H = 16
@@ -12,6 +13,34 @@
 bucket_edges = (12, 16, 23, 32, 46, 64, 91)
 norm_eps = 1e-06
 highest = lax.Precision.HIGHEST
+
+
+def derive_the_flows(v0, chip_axis):
+    block_next, met_up, ready = (axis_size(chip_axis), axis_index(chip_axis), v0.shape[1])
+    o_now = lax.dynamic_update_slice_in_dim(
+        jnp.zeros(
+            [num * block_next if to_i == 1 else num for to_i, num in enumerate(v0.shape)], v0.dtype
+        ),
+        v0,
+        met_up * ready,
+        axis=1,
+    )
+    high = wide_out = v0
+    for p in range(1, block_next // 2 + 1):
+        high = ppermute(
+            high, chip_axis, [(to_i, (to_i + 1) % block_next) for to_i in range(block_next)]
+        )
+        o_now = lax.dynamic_update_slice_in_dim(
+            o_now, high, (met_up - p) % block_next * ready, axis=1
+        )
+        if 2 * p < block_next:
+            wide_out = ppermute(
+                wide_out, chip_axis, [(to_i, (to_i - 1) % block_next) for to_i in range(block_next)]
+            )
+            o_now = lax.dynamic_update_slice_in_dim(
+                o_now, wide_out, (met_up + p) % block_next * ready, axis=1
+            )
+    return o_now
 
 
 def bucket_ids(query_pos, key_pos):
@@ -92,10 +121,7 @@
                 lax.all_gather(bias_table, ("dp", "expert"), axis=0, tiled=True),
                 lax.all_gather(router, ("dp", "expert"), axis=0, tiled=True),
             ),
-            (
-                lax.all_gather(w_in, "dp", axis=1, tiled=True),
-                lax.all_gather(w_down, "dp", axis=1, tiled=True),
-            ),
+            (lax.all_gather(w_in, "dp", axis=1, tiled=True), derive_the_flows(w_down, "dp")),
         )
         gains_f = gains.astype(jnp.float32)
         table = table_flat.astype(jnp.float32).reshape(BUCKETS, H)

time: 1750 us -> 1740 us (level)
  waiting for transfers between devices: 955 us -> 902 us
  starting transfers between devices: 36 us -> 58.6 us
    all_gather x1 -> x0, waiting for transfers between devices: 79 us -> none  [local(): lax.all_gather(w_down, 'dp', axis=1, tiled=True)]
    ppermute x0 -> x7, waiting for transfers between devices: none -> 64.5 us  [the longest x3 58 us: derive_the_flows(): ppermute(wide_out, chip_axis, [(to_i, (to_i - 1) % block_next) for to_i i...]
    all_gather x1, waiting for transfers between devices: 42.5 us -> 0.02 us  [local(): lax.all_gather(w_in, 'dp', axis=1, tiled=True)]
    ppermute x0 -> x7, starting transfers between devices: none -> 22.7 us  [the longest x4 13.8 us: derive_the_flows(): ppermute(high, chip_axis, [(to_i, (to_i + 1) % block_next) for to_i in ra...]
    unnamed x20 -> x19, waiting for transfers between devices: 114 us -> 113 us
  transfers between devices with their start and end apart: 26 -> 32, of which waited for: 16 -> 19; matrix products, arithmetic and copies ran while one was open for 27% -> 28% of each run, Pallas kernels for 0% -> 0%
where the time goes in v1:
time: 1740 us; the launch traced here: 1730 us
  waiting for transfers between devices  902 us (52%)
  matrix products  398 us (23%)
  blocking collectives  168 us (10%)
  local copies, waits for them, and re-layouts  122 us (7%)
  other arithmetic  67.2 us (4%)
  starting transfers between devices  58.6 us (3%)
    reduce_scatter x1, waiting for transfers between devices, local(): lax.psum_scatter(acc_in[None].astype(jnp.bfloat16), 'dp', scatter_dimensi...  193 us
    reduce_scatter x1, waiting for transfers between devices, local(): lax.psum_scatter(acc_qkv, ('dp', 'expert'), scatter_dimension=0, tiled=True)  157 us
    reduce_scatter x1, waiting for transfers between devices, local(): lax.psum_scatter(acc_out, ('dp', 'expert'), scatter_dimension=0, tiled=True)  141 us
    unnamed x19, waiting for transfers between devices  113 us
    reduce_scatter x1, waiting for transfers between devices, local(): lax.psum_scatter(acc_down[None].astype(jnp.bfloat16), 'dp', scatter_dimen...  109 us
    dot_general x10, matrix products, times_trans(): jnp.einsum('ti,ji->tj', left, right, preferred_element_type=jnp.float32)  88.4 us
    dot_general x10, matrix products, inner_rows(): jnp.einsum('ti,tj->ij', left, right, preferred_element_type=jnp.float32)  79 us
    unnamed x2, blocking collectives  77.6 us
  transfers between devices with their start and end apart: 32, of which 19 were waited for; matrix products, arithmetic and copies ran while one was open for 28% of the time, Pallas kernels for 0%

profile of v1, /device:TPU:0, one launch (start us, length us, event | category | flops | bytes accessed | tf_op | source)
XLA Modules:
  0.0 1730.7 jit_solution(17359545642670387388)
XLA Ops:
  8.0 43.5 %all-gather = bf16[32,32,2]{1,2,0:T(2,128)(2,1)S(1)} all-gather(bf16[1,32,2]{1,2,0:T(2,128)(2,1)} %bitcast.312), channel_id=1, replica_groups=mesh['dp'=8,'expert'=4] {'dp','expert'}, dimensions={0}, use_global_device_ids=true | all-gather | bytes 4224 | tf_op jit(solution)/shard_map/all_gather | solution.py:120
  53.6 29.3 %all-gather.10.cloned.1.call-done = bf16[1024,3072]{1,0:T(8,128)(2,1)} async-done(((bf16[32,3072]{1,0:T(8,128)(2,1)}), bf16[1024,3072]{1,0:T(8,128)(2,1)}) %all-gather.10.cloned.1.call-update) | async-done | bytes 6291472 | tf_op jit(solution)/shard_map/all_gather | solution.py:118
  112.4 46.0 %copy.135 = pred[256,1024,32]{1,2,0:T(32,128)(4,1)} copy(pred[256,1024,32]{0,2,1:T(32,128)(4,1)} %iota_compare_fusion) | data formatting | bytes 16777216 | tf_op jit(solution)/shard_map/eq | solution.py:102
  158.7 38.2 %all-reduce.4 = bf16[512]{0:T(512)(128)(2,1)S(1)} all-reduce(bf16[512]{0:T(512)(128)(2,1)S(1)} %dynamic-update-slice), channel_id=1, replica_groups=mesh['dp'=8,'expert'=4] {'dp','expert'}, use_global_device_ids=true, to_apply=%add.4 | all-reduce | flops 512 | bytes 2048
  220.8 46.8 %all-gather.1 = bf16[32,32,4]{1,2,0:T(4,128)(2,1)S(1)} all-gather(bf16[1,32,4]{1,2,0:T(4,128)(2,1)S(1)} %bitcast.311), channel_id=1, replica_groups=mesh['dp'=8,'expert'=4] {'dp','expert'}, dimensions={0}, use_global_device_ids=true | all-gather | bytes 8448 | tf_op jit(solution)/shard_map/all_gather | solution.py:122
  281.9 21.0 %collective-permute-done.3 = bf16[1,352,1024]{2,1,0:T(8,128)(2,1)S(1)} collective-permute-done((bf16[1,352,1024]{2,1,0:T(8,128)(2,1)}, bf16[1,352,1024]{2,1,0:T(8,128)(2,1)S(1)}, u32[]{:S(2)}, u32[]{:S(2)}) %collective-permute-start.3) | collective-permute-done | bytes 720928 | tf_op jit(solution)/shard_map/ppermute | solution.py:37
  323.2 37.0 %collective-permute-done.5 = bf16[1,352,1024]{2,1,0:T(8,128)(2,1)S(1)} collective-permute-done((bf16[1,352,1024]{2,1,0:T(8,128)(2,1)S(1)}, bf16[1,352,1024]{2,1,0:T(8,128)(2,1)S(1)}, u32[]{:S(2)}, u32[]{:S(2)}) %collective-permute-start.5) | collective-permute-done | bytes 720928 | tf_op jit(solution)/shard_map/ppermute | solution.py:37
  374.3 22.4 %fusion.157 = (f32[16,256]{1,0:T(8,128)S(1)}, f32[16,256,1024]{2,1,0:T(8,128)}) fusion(f32[16,256,1024]{2,0,1:T(8,128)} %fusion.128, bf16[256,16,64]{0,2,1:T(8,128)(2,1)} %bitcast.263, bf16[1024,16,64]{0,2,1:T(8,128)(2,1)S(1)} %bitcast.253, pred[1024]{0:T(1024)(128)(4,1)S(1)} %iota_compare_fusion.22), kind=kOutput, calls=%fused_computation.267 | convolution fusion | flops 553644032 | bytes 36193280 | tf_op jit(solution)/shard_map/qhd,khd->hqk/dot_general | solution.py:146
  427.0 22.4 %fusion.159 = (f32[16,256]{1,0:T(8,128)S(1)}, f32[16,256,1024]{2,1,0:T(8,128)}) fusion(f32[16,256,1024]{2,0,1:T(8,128)} %fusion.128, bf16[256,16,64]{0,2,1:T(8,128)(2,1)} %bitcast.265, bf16[1024,16,64]{0,2,1:T(8,128)(2,1)S(1)} %bitcast.255, pred[1024]{0:T(1024)(128)(4,1)S(1)} %iota_compare_fusion.21), kind=kOutput, calls=%fused_computation.269 | convolution fusion | flops 553644032 | bytes 36193280 | tf_op jit(solution)/shard_map/qhd,khd->hqk/dot_general | solution.py:146
  486.3 18.8 %fusion.28 = (f32[640,2816]{1,0:T(8,128)}, f32[640,2816]{1,0:T(8,128)}, bf16[640,2816]{1,0:T(8,128)(2,1)}) fusion(f32[640,5632]{1,0:T(8,128)} %fusion.12, bf16[640,1024]{1,0:T(8,128)(2,1)S(1)} %bitcast.285, bf16[2816,1024]{1,0:T(8,128)(2,1)} %bitcast_dynamic-update-slice_fusion), kind=kOutput, calls=%fused_computation.59 | convolution fusion | flops 3734241280 | bytes 39518208 | tf_op jit(solution)/shard_map/ti,ji->tj/dot_general | solution.py:88
  505.1 15.5 fusion.52
  600.3 13.8 fusion.10
  617.6 17.9 %fusion.29 = (f32[640,2816]{1,0:T(8,128)}, f32[640,2816]{1,0:T(8,128)}, bf16[640,2816]{1,0:T(8,128)(2,1)}) fusion(f32[640,5632]{1,0:T(8,128)} %fusion.10, bf16[640,1024]{1,0:T(8,128)(2,1)} %bitcast.65, bf16[2816,1024]{1,0:T(8,128)(2,1)} %bitcast_dynamic-update-slice_fusion), kind=kOutput, calls=%fused_computation.60 | convolution fusion | flops 3734241280 | bytes 39518208 | tf_op jit(solution)/shard_map/ti,ji->tj/dot_general | solution.py:88
  635.5 15.5 fusion.55
  680.1 14.3 all-to-all-done.3
  810.2 34.3 %reduce-scatter.15.cloned.1.call-done = bf16[256,1024]{0,1:T(8,128)(2,1)} async-done(((bf16[1024,1024]{0,1:T(8,128)(2,1)}), bf16[256,1024]{0,1:T(8,128)(2,1)}) %reduce-scatter.15.cloned.1.call-update) | async-done | bytes 524304 | tf_op jit(solution)/shard_map/reduce_scatter | solution.py:268
  865.3 19.0 %fusion.105 = f32[1024,5632]{1,0:T(8,128)} fusion(bf16[640,1024]{1,0:T(8,128)(2,1)} %bitcast.17, f32[640,2816]{1,0:T(8,128)} %get-tuple-element.26, f32[640,2816]{1,0:T(8,128)} %get-tuple-element.25), kind=kOutput, calls=%fused_computation.163 | convolution fusion | flops 7389184000 | bytes 38797312 | tf_op jit(solution)/shard_map/ti,tj->ij/dot_general | solution.py:84
  884.3 21.2 %fusion.14 = bf16[1,1024,5632]{2,1,0:T(8,128)(2,1)} fusion(f32[1024,5632]{1,0:T(8,128)} %fusion.105, bf16[640,1024]{1,0:T(8,128)(2,1)} %bitcast.43, f32[640,2816]{1,0:T(8,128)} %get-tuple-element.28, f32[640,2816]{1,0:T(8,128)} %get-tuple-element.27), kind=kOutput, calls=%fused_computation.33 | convolution fusion | flops 7400718336 | bytes 50331648 | tf_op jit(solution)/shard_map/ti,tj->ij/dot_general | solution.py:84
  960.2 39.4 %all-reduce.5 = f32[512]{0:T(512)S(1)} all-reduce(f32[512]{0:T(512)S(1)} %reshape.503), channel_id=9, replica_groups=mesh['dp'=8,'expert'=4] {'dp','expert'}, use_global_device_ids=true, to_apply=%region_47.48.clone | all-reduce | flops 512 | bytes 4096
  1007.5 109.5 %reduce-scatter.31.cloned.1.call-done = f32[32,2]{1,0:T(8,128)} async-done(((f32[1024,2]{1,0:T(8,128)}), f32[32,2]{1,0:T(8,128)}) %reduce-scatter.31.cloned.1.call-update) | async-done | bytes 272
  1118.4 108.7 %reduce-scatter.29.cloned.1.call-done = bf16[1,352,1024]{2,1,0:T(8,128)(2,1)} async-done(((bf16[1,2816,1024]{2,1,0:T(8,128)(2,1)}), bf16[1,352,1024]{2,1,0:T(8,128)(2,1)}) %reduce-scatter.29.cloned.1.call-update) | async-done | bytes 720912 | tf_op jit(solution)/shard_map/reduce_scatter | solution.py:308
  1229.5 193.3 %reduce-scatter.27.cloned.1.call-done = bf16[1,128,5632]{2,1,0:T(8,128)(2,1)} async-done(((bf16[1,1024,5632]{2,1,0:T(8,128)(2,1)}), bf16[1,128,5632]{2,1,0:T(8,128)(2,1)}) %reduce-scatter.27.cloned.1.call-update) | async-done | bytes 1441808 | tf_op jit(solution)/shard_map/reduce_scatter | solution.py:305
  1426.0 140.8 %reduce-scatter.25.cloned.1.call-done = f32[32,1024]{1,0:T(8,128)} async-done(((f32[1024,1024]{1,0:T(8,128)}), f32[32,1024]{1,0:T(8,128)}) %reduce-scatter.25.cloned.1.call-update) | async-done | bytes 131088 | tf_op jit(solution)/shard_map/reduce_scatter | solution.py:297
  1566.8 157.2 %reduce-scatter.23.cloned.1.call-done = f32[32,3072]{1,0:T(8,128)} async-done(((f32[1024,3072]{1,0:T(8,128)}), f32[32,3072]{1,0:T(8,128)}) %reduce-scatter.23.cloned.1.call-update) | async-done | bytes 393232 | tf_op jit(solution)/shard_map/reduce_scatter | solution.py:296
  (399 shorter events, 489.1 us)
Async XLA Ops:
  7.2 75.8 %all-gather.10.cloned.1.call-start = ((), (), s32[]{:S(2)}) async-start(), calls=%async_computation.18 | async-start | bytes 6488064 | tf_op jit(solution)/shard_map/all_gather | solution.py:118
  7.9 359.6 %all-gather.12.cloned.1.call-start = ((), (), s32[]{:S(2)}) async-start(), calls=%async_computation.19 | async-start | bytes 2621440 | tf_op jit(solution)/shard_map/all_gather | solution.py:138
  89.0 282.4 %all-gather.14.cloned.1.call-start = ((), (), s32[]{:S(2)}) async-start(), calls=%async_computation.20 | async-start | bytes 2621440 | tf_op jit(solution)/shard_map/all_gather | solution.py:137
  89.7 323.5 %all-gather.16.cloned.1.call-start = ((), (), s32[]{:S(2)}) async-start(), calls=%async_computation.21 | async-start | bytes 2162688 | tf_op jit(solution)/shard_map/all_gather | solution.py:119
  90.3 333.8 %all-gather.22.cloned.1.call-start = ((), (), s32[]{:S(2)}) async-start(), calls=%async_computation.24 | async-start | bytes 2621440 | tf_op jit(solution)/shard_map/all_gather | solution.py:137
  96.3 361.3 %all-gather.20.cloned.1.call-start = ((), (), s32[]{:S(2)}) async-start(), calls=%async_computation.23 | async-start | bytes 2621440 | tf_op jit(solution)/shard_map/all_gather | solution.py:138
  96.9 372.3 %all-gather.18.cloned.1.call-start = ((), (), s32[]{:S(2)}) async-start(), calls=%async_computation.22 | async-start | bytes 12976128 | tf_op jit(solution)/shard_map/all_gather | solution.py:124
  97.6 120.1 %collective-permute-start = (bf16[1,352,1024]{2,1,0:T(8,128)(2,1)}, bf16[1,352,1024]{2,1,0:T(8,128)(2,1)}, u32[]{:S(2)}, u32[]{:S(2)}) collective-permute-start(bf16[1,352,1024]{2,1,0:T(8,128)(2,1)} %param.20), channel_id=1, source_target_pairs={{0,4},{4,8},{8,12},{12,16},{16,20},{20,24},{24,28},{28,0},{1,5},{5... | collective-permute-start | bytes 2162696 | tf_op jit(solution)/shard_map/ppermute | solution.py:30
  99.1 171.4 %collective-permute-start.1 = (bf16[1,352,1024]{2,1,0:T(8,128)(2,1)}, bf16[1,352,1024]{2,1,0:T(8,128)(2,1)}, u32[]{:S(2)}, u32[]{:S(2)}) collective-permute-start(bf16[1,352,1024]{2,1,0:T(8,128)(2,1)} %param.20), channel_id=1, source_target_pairs={{0,28},{4,0},{8,4},{12,8},{16,12},{20,16},{24,20},{28,24},{1,29},{... | collective-permute-start | bytes 2162696 | tf_op jit(solution)/shard_map/ppermute | solution.py:37
  217.7 58.4 %collective-permute-start.2 = (bf16[1,352,1024]{2,1,0:T(8,128)(2,1)}, bf16[1,352,1024]{2,1,0:T(8,128)(2,1)}, u32[]{:S(2)}, u32[]{:S(2)}) collective-permute-start(bf16[1,352,1024]{2,1,0:T(8,128)(2,1)} %collective-permute-done), channel_id=1, source_target_pairs={{0,4},{4,8},{8,12},{12,16},{16,20},{20,24},{24,28},{28,0},{1,5},{5... | collective-permute-start | bytes 2162696 | tf_op jit(solution)/shard_map/ppermute | solution.py:30
  276.1 37.0 %collective-permute-start.4 = (bf16[1,352,1024]{2,1,0:T(8,128)(2,1)}, bf16[1,352,1024]{2,1,0:T(8,128)(2,1)S(1)}, u32[]{:S(2)}, u32[]{:S(2)}) collective-permute-start(bf16[1,352,1024]{2,1,0:T(8,128)(2,1)} %collective-permute-done.2), channel_id=1, source_target_pairs={{0,4},{4,8},{8,12},{12,16},{16,20},{20,24},{24,28},{28,0},{1,5},{5... | collective-permute-start | bytes 2162696 | tf_op jit(solution)/shard_map/ppermute | solution.py:30
  302.9 57.4 %collective-permute-start.5 = (bf16[1,352,1024]{2,1,0:T(8,128)(2,1)S(1)}, bf16[1,352,1024]{2,1,0:T(8,128)(2,1)S(1)}, u32[]{:S(2)}, u32[]{:S(2)}) collective-permute-start(bf16[1,352,1024]{2,1,0:T(8,128)(2,1)S(1)} %collective-permute-done.3), channel_id=1, source_target_pairs={{0,28},{4,0},{8,4},{12,8},{16,12},{20,16},{24,20},{28,24},{1,29},{... | collective-permute-start | bytes 2162696 | tf_op jit(solution)/shard_map/ppermute | solution.py:37
  313.1 51.4 %collective-permute-start.6 = (bf16[1,352,1024]{2,1,0:T(8,128)(2,1)S(1)}, bf16[1,352,1024]{2,1,0:T(8,128)(2,1)S(1)}, u32[]{:S(2)}, u32[]{:S(2)}) collective-permute-start(bf16[1,352,1024]{2,1,0:T(8,128)(2,1)S(1)} %collective-permute-done.4), channel_id=1, source_target_pairs={{0,4},{4,8},{8,12},{12,16},{16,20},{20,24},{24,28},{28,0},{1,5},{5... | collective-permute-start | bytes 2162696 | tf_op jit(solution)/shard_map/ppermute | solution.py:30
  419.6 45.8 %all-to-all-start = ((bf16[4,160,1024]{2,1,0:T(8,128)(2,1)}), bf16[4,160,1024]{2,1,0:T(8,128)(2,1)}, u32[]{:S(2)}, u32[]{:S(2)}) async-start(bf16[4,160,1024]{2,1,0:T(8,128)(2,1)} %bitcast.16), calls=%async_computation | async-start | bytes 2621440 | tf_op jit(solution)/shard_map/all_to_all | solution.py:173
  677.1 119.8 %reduce-scatter.21.cloned.1.call-start = ((), (), s32[]{:S(2)}) async-start(), calls=%async_computation.28 | async-start | bytes 2621440 | tf_op jit(solution)/shard_map/reduce_scatter | solution.py:274
  712.9 84.1 %reduce-scatter.19.cloned.1.call-start = ((), (), s32[]{:S(2)}) async-start(), calls=%async_computation.27 | async-start | bytes 2621440 | tf_op jit(solution)/shard_map/reduce_scatter | solution.py:268
  735.4 74.8 %reduce-scatter.17.cloned.1.call-start = ((), (), s32[]{:S(2)}) async-start(), calls=%async_computation.26 | async-start | bytes 2621440 | tf_op jit(solution)/shard_map/reduce_scatter | solution.py:274
  748.1 96.4 %reduce-scatter.15.cloned.1.call-start = ((), (), s32[]{:S(2)}) async-start(), calls=%async_computation.25 | async-start | bytes 2621440 | tf_op jit(solution)/shard_map/reduce_scatter | solution.py:268
  770.7 231.8 %reduce-scatter.33.cloned.1.call-start = ((), (), s32[]{:S(2)}) async-start(), calls=%async_computation.34 | async-start | bytes 540672
  796.8 320.2 %reduce-scatter.31.cloned.1.call-start = ((), (), s32[]{:S(2)}) async-start(), calls=%async_computation.33 | async-start | bytes 540672
  851.8 375.3 %reduce-scatter.29.cloned.1.call-start = ((), (), s32[]{:S(2)}) async-start(), calls=%async_computation.32 | async-start | bytes 6488064 | tf_op jit(solution)/shard_map/reduce_scatter | solution.py:308
  865.3 557.5 %reduce-scatter.27.cloned.1.call-start = ((), (), s32[]{:S(2)}) async-start(), calls=%async_computation.31 | async-start | bytes 12976128 | tf_op jit(solution)/shard_map/reduce_scatter | solution.py:305
  905.5 661.2 %reduce-scatter.25.cloned.1.call-start = ((), (), s32[]{:S(2)}) async-start(), calls=%async_computation.30 | async-start | bytes 4325376 | tf_op jit(solution)/shard_map/reduce_scatter | solution.py:297
  911.4 812.6 %reduce-scatter.23.cloned.1.call-start = ((), (), s32[]{:S(2)}) async-start(), calls=%async_computation.29 | async-start | bytes 12976128 | tf_op jit(solution)/shard_map/reduce_scatter | solution.py:296
  (90 other events, 2134.3 us)
Sparse Core Ops, SparseCore 0:
  10.9 72.0 all-gather.9
  89.1 21.0 all-gather.11
  112.4 22.5 all-gather.13
  137.7 56.4 all-gather.15
  196.2 21.4 all-gather.21
  219.2 22.6 all-gather.19
  244.0 199.9 all-gather.17
  713.0 29.2 reduce-scatter.20
  745.4 31.1 reduce-scatter.18
  779.0 31.1 reduce-scatter.16
  813.3 31.1 reduce-scatter.14
  846.5 135.8 reduce-scatter.32
  985.2 131.7 reduce-scatter.30
  1120.5 106.5 reduce-scatter.28
  1230.5 192.1 reduce-scatter.26
  1425.4 141.2 reduce-scatter.24
  1573.2 150.7 reduce-scatter.22
